TPU v7x, 32 devices: a whole 2x2x4 slice. The times are simulated.
32 devices in a mesh: dp: 16 (over z, y, x), mp: 2 (over core).
Axes of the slice: x: 2, y: 2, z: 4, core: 2. Of those that a mesh axis runs over, the one named last changes fastest.
Arguments:
- tokens: bfloat16 [32768, 768], P(('dp', 'mp')), may hold values from -6 to 6
- w_query: bfloat16 [768, 768], P('dp', 'mp'), may hold values from -0.625 to 0.625
- w_key: bfloat16 [768, 768], P('dp', 'mp'), may hold values from -0.625 to 0.625
- w_value: bfloat16 [768, 768], P('dp', 'mp'), may hold values from -0.21875 to 0.21875
- value_taps: float32 [12, 33], P('mp'), may hold values from -0.3 to 0.3
- w_output: bfloat16 [768, 768], P(None, ('dp', 'mp')), may hold values from -0.875 to 0.875
- first_gain: bfloat16 [768], P(('dp', 'mp')), may hold values from 0.25 to 1.75
- first_bias: bfloat16 [768], P(('dp', 'mp')), may hold values from -1.5 to 1.5
- w_expand: bfloat16 [768, 3072], P('dp', 'mp'), may hold values from -0.21875 to 0.21875
- w_shrink: bfloat16 [3072, 768], P('mp', 'dp'), may hold values from -0.21875 to 0.21875
- second_gain: bfloat16 [768], P(('dp', 'mp')), may hold values from 0.25 to 1.75
- second_bias: bfloat16 [768], P(('dp', 'mp')), may hold values from -1.5 to 1.5
- doc_lengths: int32 [32], replicated, may hold values from 256 to 1024, as said below
- out_grad: bfloat16 [32768, 768], P(('dp', 'mp')), may hold values from -6 to 6
Outputs:
- layer_out: bfloat16 [32768, 768], P(('dp', 'mp'))
- tokens_grad: float32 [32768, 768], P(('dp', 'mp'))
- query_grad: float32 [768, 768], P('dp', 'mp')
- key_grad: float32 [768, 768], P('dp', 'mp')
- value_grad: float32 [768, 768], P('dp', 'mp')
- taps_grad: float32 [12, 33], P('mp')
- output_grad: float32 [768, 768], P(None, ('dp', 'mp'))
- first_gain_grad: float32 [768], P(('dp', 'mp'))
- first_bias_grad: float32 [768], P(('dp', 'mp'))
- expand_grad: float32 [768, 3072], P('dp', 'mp')
- shrink_grad: float32 [3072, 768], P('mp', 'dp')
- second_gain_grad: float32 [768], P(('dp', 'mp'))
- second_bias_grad: float32 [768], P(('dp', 'mp'))
Inputs may be any that keep to these rules, and one draw needn't show every extreme that they name: Document i occupies the first doc_lengths[i] positions of slot i of 1024 positions; the rest is padding. In every draw some document fills its whole slot.
All inputs are finite; a program needn't handle non-finite values.
Results may differ from a plain program's by a relative error of at most 0.018.
The roundings to bfloat16 on the way count: a program that leaves them out, or rounds other values in their place, can miss the bound.
Values may be sent and summed in bfloat16 or wider, within the bound.
A program may use at most 320 MiB of HBM per device.

v0:
```python
import jax
import jax.numpy as jnp
from jax import lax
from jax.sharding import PartitionSpec as P

HEAD_DIM = 64
LANDMARKS = 64
KERNEL = 33
PINV_STEPS = 6
HIGH = lax.Precision.HIGHEST


def ahead(left, right):
    return jnp.dot(left, right, preferred_element_type=jnp.float32)


def against(left, right):
    return lax.dot_general(
        left, right, (((1,), (1,)), ((), ())), preferred_element_type=jnp.float32
    )


def across(left, right):
    return lax.dot_general(
        left, right, (((0,), (0,)), ((), ())), preferred_element_type=jnp.float32
    )


def layer_norm(values, gain, bias):
    middle = jnp.mean(values, axis=-1, keepdims=True)
    centered = values - middle
    variance = jnp.mean(centered * centered, axis=-1, keepdims=True)
    return centered * lax.rsqrt(variance + 1e-05) * gain + bias


def exact_gelu(values):
    return jax.nn.gelu(values, approximate=False)


def inverse_estimate(matrix):
    widest = jnp.max(jnp.sum(matrix, axis=-2), axis=-1)
    current = jnp.swapaxes(matrix, -1, -2) / widest[:, None, None]
    identity = jnp.eye(matrix.shape[-1], dtype=jnp.float32)[None]
    for step in range(PINV_STEPS):
        product = jnp.einsum("hij,hjk->hik", matrix, current, precision=HIGH)
        inner_term = 7.0 * identity - product
        inner_term = 15.0 * identity - jnp.einsum(
            "hij,hjk->hik", product, inner_term, precision=HIGH
        )
        inner_term = 13.0 * identity - jnp.einsum(
            "hij,hjk->hik", product, inner_term, precision=HIGH
        )
        current = 0.25 * jnp.einsum("hij,hjk->hik", current, inner_term, precision=HIGH)
    return current


def nystrom(query, keys, values, taps, length):
    slots = query.shape[0]
    positions = jnp.arange(slots, dtype=jnp.int32)
    valid = positions < length
    weight = valid.astype(jnp.float32)
    segment = positions * LANDMARKS // length
    member = (
        (segment[None, :] == jnp.arange(LANDMARKS, dtype=jnp.int32)[:, None]) & valid[None, :]
    ).astype(jnp.float32)
    member = member / jnp.sum(member, axis=1, keepdims=True)
    mark_query = jnp.einsum("js,shd->hjd", member, query, precision=HIGH)
    mark_keys = jnp.einsum("js,shd->hjd", member, keys, precision=HIGH)
    scale = HEAD_DIM ** (-0.5)
    first = jax.nn.softmax(
        jnp.einsum("shd,hjd->hsj", query, mark_keys, precision=HIGH) * scale, axis=-1
    )
    second = jax.nn.softmax(
        jnp.einsum("hid,hjd->hij", mark_query, mark_keys, precision=HIGH) * scale, axis=-1
    )
    third_scores = jnp.einsum("hjd,shd->hjs", mark_query, keys, precision=HIGH) * scale
    third = jax.nn.softmax(jnp.where(valid[None, None, :], third_scores, -1e30), axis=-1)
    inverse = inverse_estimate(second)
    summary = jnp.einsum("hjs,shd->hjd", third, values, precision=HIGH)
    carried = jnp.einsum("hij,hjd->hid", inverse, summary, precision=HIGH)
    mixed = jnp.einsum("hsj,hjd->shd", first, carried, precision=HIGH)
    radius = KERNEL // 2
    padded = jnp.pad(values * weight[:, None, None], ((radius, radius), (0, 0), (0, 0)))
    for index in range(KERNEL):
        mixed = mixed + taps[:, index][None, :, None] * padded[index : index + slots]
    mixed = mixed * weight[:, None, None]
    return mixed.reshape(slots, query.shape[1] * HEAD_DIM)


def on_device(
    tokens,
    w_query,
    w_key,
    w_value,
    value_taps,
    w_output,
    first_gain,
    first_bias,
    w_expand,
    w_shrink,
    second_gain,
    second_bias,
    doc_lengths,
    out_grad,
):
    parts = lax.axis_size("mp")
    group = lax.axis_index("dp")
    slots = tokens.shape[0]
    pair = lax.dynamic_slice_in_dim(doc_lengths, group * parts, parts)
    full_query, full_keys, full_values, full_expand, full_shrink = (
        lax.all_gather(w_query, "dp", axis=0, tiled=True),
        lax.all_gather(w_key, "dp", axis=0, tiled=True),
        lax.all_gather(w_value, "dp", axis=0, tiled=True),
        lax.all_gather(w_expand, "dp", axis=0, tiled=True),
        lax.all_gather(w_shrink, "dp", axis=1, tiled=True),
    )
    full_output, gain_one, bias_one, gain_two, bias_two = (
        lax.all_gather(w_output, ("dp", "mp"), axis=1, tiled=True),
        lax.all_gather(first_gain, ("dp", "mp"), axis=0, tiled=True),
        lax.all_gather(first_bias, ("dp", "mp"), axis=0, tiled=True),
        lax.all_gather(second_gain, ("dp", "mp"), axis=0, tiled=True),
        lax.all_gather(second_bias, ("dp", "mp"), axis=0, tiled=True),
    )
    gain_one = gain_one.astype(jnp.float32)
    bias_one = bias_one.astype(jnp.float32)
    gain_two = gain_two.astype(jnp.float32)
    bias_two = bias_two.astype(jnp.float32)
    local_heads = full_query.shape[1] // HEAD_DIM
    grouped = lax.all_gather(tokens, "mp", axis=0, tiled=True)
    query_low = ahead(grouped, full_query).astype(jnp.bfloat16)
    keys_low = ahead(grouped, full_keys).astype(jnp.bfloat16)
    values_low = ahead(grouped, full_values).astype(jnp.bfloat16)

    def attention_core(query, keys, values, taps):
        shape = (parts, slots, local_heads, HEAD_DIM)
        mixed = jax.vmap(nystrom, in_axes=(0, 0, 0, None, 0))(
            query.reshape(shape), keys.reshape(shape), values.reshape(shape), taps, pair
        )
        return mixed.reshape(parts * slots, local_heads * HEAD_DIM)

    attended, core_back = jax.vjp(
        attention_core,
        query_low.astype(jnp.float32),
        keys_low.astype(jnp.float32),
        values_low.astype(jnp.float32),
        value_taps,
    )
    attended_tok = lax.all_to_all(
        attended.astype(jnp.bfloat16), "mp", split_axis=0, concat_axis=1, tiled=True
    )
    projected = ahead(attended_tok, full_output)
    first_out, first_back = jax.vjp(
        layer_norm, tokens.astype(jnp.float32) + projected, gain_one, bias_one
    )
    hidden_all = lax.all_gather(first_out.astype(jnp.bfloat16), "mp", axis=0, tiled=True)
    pre = ahead(hidden_all, full_expand)
    active, gelu_back = jax.vjp(exact_gelu, pre)
    active_low = active.astype(jnp.bfloat16)
    branch = lax.psum_scatter(
        ahead(active_low, full_shrink).astype(jnp.bfloat16), "mp", scatter_dimension=0, tiled=True
    ).astype(jnp.float32)
    result, second_back = jax.vjp(layer_norm, first_out + branch, gain_two, bias_two)
    layer_out = result.astype(jnp.bfloat16)
    d_second_in, gain_two_grad, bias_two_grad = second_back(out_grad.astype(jnp.float32))
    branch_grad = lax.all_gather(d_second_in.astype(jnp.bfloat16), "mp", axis=0, tiled=True)
    back_query, back_keys, back_values, back_expand, back_shrink = (
        lax.all_gather(w_query, "dp", axis=0, tiled=True),
        lax.all_gather(w_key, "dp", axis=0, tiled=True),
        lax.all_gather(w_value, "dp", axis=0, tiled=True),
        lax.all_gather(w_expand, "dp", axis=0, tiled=True),
        lax.all_gather(w_shrink, "dp", axis=1, tiled=True),
    )
    (d_pre,) = gelu_back(against(branch_grad, back_shrink))
    d_pre_low = d_pre.astype(jnp.bfloat16)
    shrink_grad = across(active_low, branch_grad)
    expand_grad = across(hidden_all, d_pre_low)
    d_hidden = lax.psum_scatter(
        against(d_pre_low, back_expand).astype(jnp.bfloat16), "mp", scatter_dimension=0, tiled=True
    ).astype(jnp.float32)
    d_first_in, gain_one_grad, bias_one_grad = first_back(d_second_in + d_hidden)
    d_projected = d_first_in.astype(jnp.bfloat16)
    output_grad = across(attended_tok, d_projected)
    d_attended = against(d_projected, full_output).astype(jnp.bfloat16)
    d_heads = lax.all_to_all(d_attended, "mp", split_axis=1, concat_axis=0, tiled=True)
    d_query, d_keys, d_values, taps_grad = core_back(d_heads.astype(jnp.float32))
    d_query = d_query.astype(jnp.bfloat16)
    d_keys = d_keys.astype(jnp.bfloat16)
    d_values = d_values.astype(jnp.bfloat16)
    query_grad = across(grouped, d_query)
    key_grad = across(grouped, d_keys)
    value_grad = across(grouped, d_values)
    total = against(d_query, back_query)
    total = total + against(d_keys, back_keys)
    tokens_grad = d_first_in + lax.psum_scatter(
        (total + against(d_values, back_values)).astype(jnp.bfloat16),
        "mp",
        scatter_dimension=0,
        tiled=True,
    ).astype(jnp.float32)
    query_grad, key_grad, value_grad, expand_grad, shrink_grad = (
        lax.psum_scatter(query_grad, "dp", scatter_dimension=0, tiled=True),
        lax.psum_scatter(key_grad, "dp", scatter_dimension=0, tiled=True),
        lax.psum_scatter(value_grad, "dp", scatter_dimension=0, tiled=True),
        lax.psum_scatter(expand_grad, "dp", scatter_dimension=0, tiled=True),
        lax.psum_scatter(shrink_grad, "dp", scatter_dimension=1, tiled=True),
    )
    output_grad, gain_one_grad, bias_one_grad, gain_two_grad, bias_two_grad = (
        lax.psum_scatter(output_grad, ("dp", "mp"), scatter_dimension=1, tiled=True),
        lax.psum_scatter(gain_one_grad, ("dp", "mp"), scatter_dimension=0, tiled=True),
        lax.psum_scatter(bias_one_grad, ("dp", "mp"), scatter_dimension=0, tiled=True),
        lax.psum_scatter(gain_two_grad, ("dp", "mp"), scatter_dimension=0, tiled=True),
        lax.psum_scatter(bias_two_grad, ("dp", "mp"), scatter_dimension=0, tiled=True),
    )
    taps_grad = lax.psum(taps_grad, "dp")
    return (
        layer_out,
        tokens_grad,
        query_grad,
        key_grad,
        value_grad,
        taps_grad,
        output_grad,
        gain_one_grad,
        bias_one_grad,
        expand_grad,
        shrink_grad,
        gain_two_grad,
        bias_two_grad,
    )


def solution(mesh):
    in_specs = (
        P(("dp", "mp"), None),
        P("dp", "mp"),
        P("dp", "mp"),
        P("dp", "mp"),
        P("mp", None),
        P(None, ("dp", "mp")),
        P(("dp", "mp")),
        P(("dp", "mp")),
        P("dp", "mp"),
        P("mp", "dp"),
        P(("dp", "mp")),
        P(("dp", "mp")),
        P(),
        P(("dp", "mp"), None),
    )
    out_specs = (
        P(("dp", "mp"), None),
        P(("dp", "mp"), None),
        P("dp", "mp"),
        P("dp", "mp"),
        P("dp", "mp"),
        P("mp", None),
        P(None, ("dp", "mp")),
        P(("dp", "mp")),
        P(("dp", "mp")),
        P("dp", "mp"),
        P("mp", "dp"),
        P(("dp", "mp")),
        P(("dp", "mp")),
    )
    return jax.shard_map(
        on_device, mesh=mesh, in_specs=in_specs, out_specs=out_specs, check_vma=False
    )
```

profile of v0, /device:TPU:0, one launch (start us, length us, event | category | flops | bytes accessed | tf_op | source)
XLA Modules:
  0.0 1484.3 jit_solution(6945524106746862283)
XLA Ops:
  18.9 42.1 %all-reduce.76 = (bf16[768]{0:T(1024)(128)(2,1)S(1)}, bf16[768]{0:T(1024)(128)(2,1)S(1)}, bf16[768]{0:T(1024)(128)(2,1)}, bf16[768]{0:T(1024)(128)(2,1)}) all-reduce(bf16[768]{0:T(1024)(128)(2,1)S(1)} %dynamic-update-slice.1, bf16[768]{0:T(1024)(128)(2,1)S(1)} %dynamic-update-slice, ...), channel_id=1, replica_groups=mesh['dp'=16,'mp'=2] {'dp','mp'}, use_global_device_ids=true, to_apply=%add.68 | all-reduce | flops 3072 | bytes 12288
  62.4 44.0 %all_gather.45 = bf16[768,384]{1,0:T(8,128)(2,1)S(1)} all-gather(bf16[48,384]{1,0:T(8,128)(2,1)S(1)} %copy-done.119), channel_id=1, replica_groups=mesh['dp'=16,'mp'=2] {'dp'}, dimensions={0}, use_global_device_ids=true | all-gather | bytes 626688 | tf_op jit(solution)/shard_map/all_gather | solution.py:111
  106.3 41.1 %all_gather.46 = bf16[768,384]{1,0:T(8,128)(2,1)S(1)} all-gather(bf16[48,384]{1,0:T(8,128)(2,1)S(1)} %copy-done.120), channel_id=1, replica_groups=mesh['dp'=16,'mp'=2] {'dp'}, dimensions={0}, use_global_device_ids=true | all-gather | bytes 626688 | tf_op jit(solution)/shard_map/all_gather | solution.py:112
  147.4 43.7 %all_gather.47 = bf16[768,384]{1,0:T(8,128)(2,1)} all-gather(bf16[48,384]{1,0:T(8,128)(2,1)S(1)} %copy-done.121), channel_id=1, replica_groups=mesh['dp'=16,'mp'=2] {'dp'}, dimensions={0}, use_global_device_ids=true | all-gather | bytes 626688 | tf_op jit(solution)/shard_map/all_gather | solution.py:113
  267.9 29.7 %multiply_convert_fusion.1 = bf16[2,1024,6,64]{1,3,2,0:T(8,128)(2,1)} fusion(f32[2,1024,6,64]{1,3,2,0:T(8,128)S(1)} %copy_multiply_fusion, f32[2,6,64,64]{3,2,1,0:T(8,128)S(1)} %fusion.157, f32[6]{0:T(128)S(1)} %copy-done.146, f32[6]{0:T(128)S(1)} %copy-done.156, f32[6]{0:T(128)S(1)} %copy-done.158, f32[6]{0:T(128)S(1)} %copy-done.160, ...), kind=kOutput, calls=%fused_computation.121 | convolution fusion | flops 659816448 | bytes 8168216 | tf_op jit(solution)/shard_map/jvp(vmap(hsj,hjd->shd))/dot_general | solution.py:81
  311.6 7.5 all-gather.11.cloned.1.call-done
  319.1 35.5 %multiply_convert_fusion = (bf16[2048,1536]{1,0:T(8,128)(2,1)}, f32[2048,1536]{1,0:T(8,128)}, f32[2048,1536]{1,0:T(8,128)}) fusion(bf16[2048,768]{0,1:T(8,128)(2,1)} %all-gather.11.cloned.1.call-done, bf16[768,1536]{1,0:T(8,128)(2,1)} %all-gather.13.cloned.1.call-done), kind=kOutput, calls=%fused_computation.3 | convolution fusion | flops 5036310528 | bytes 36962304 | tf_op jit(solution)/shard_map/dot_general | solution.py:14
  354.6 30.5 %all-gather.15.cloned.1.call-done = bf16[1536,768]{0,1:T(8,128)(2,1)} async-done(((bf16[1536,48]{0,1:T(8,128)(2,1)}), bf16[1536,768]{0,1:T(8,128)(2,1)}) %all-gather.15.cloned.1.call-update) | async-done | bytes 2359312 | tf_op jit(solution)/shard_map/all_gather | solution.py:115
  385.1 9.1 convolution_convert_fusion.1
  397.4 6.2 reduce-scatter.16.cloned.1.call-done
  415.1 13.5 all-gather.17.cloned.1.call-done
  428.6 17.3 %add_convert_fusion = bf16[2048,1536]{1,0:T(8,128)(2,1)S(1)} fusion(f32[2048,1536]{1,0:T(8,128)} %get-tuple-element.153, f32[2048,1536]{1,0:T(8,128)} %get-tuple-element.200, bf16[2048,768]{0,1:T(8,128)(2,1)} %all-gather.17.cloned.1.call-done, bf16[1536,768]{0,1:T(8,128)(2,1)} %all-gather.15.cloned.1.call-done), kind=kOutput, calls=%fused_computation.2 | convolution fusion | flops 4875878400 | bytes 36962304 | tf_op jit(solution)/shard_map/dot_general | solution.py:18
  448.6 6.4 convolution_convert_fusion
  459.4 8.0 reduce-scatter.18.cloned.1.call-done
  486.2 5.6 fusion.15
  534.2 15.2 %multiply_reduce_fusion.32 = (f32[6]{0:T(128)}, f32[6]{0:T(128)}, f32[6]{0:T(128)}, f32[6]{0:T(128)}, f32[6]{0:T(128)}, /*index=5*/f32[6]{0:T(128)}, f32[6]{0:T(...) fusion(f32[2,1024,6,64]{1,3,2,0:T(8,128)S(1)} %copy-done.5, ...), kind=kLoop, calls=%fused_computation.107 | loop fusion | flops 25952166 | bytes 12591512 | tf_op jit(solution)/shard_map/transpose(jvp(vmap()))/reduce_sum | solution.py:85
  549.6 16.9 %broadcast_multiply_fusion.1 = (f32[2,1024,6,64]{1,3,2,0:T(8,128)}, f32[2,1024,6,64]{1,3,2,0:T(8,128)}, f32[2,1024,6,64]{1,3,2,0:T(8,128)}, f32[2,1024,6,64]{1,3...) fusion(f32[6]{0:T(128)S(1)} %copy-done.157, ...), kind=kLoop, calls=%fused_computation.168 | loop fusion | flops 11796480 | bytes 47194448 | tf_op jit(solution)/shard_map/transpose(jvp(vmap()))/mul | solution.py:85
  566.5 21.3 %broadcast_multiply_fusion = (f32[2,1024,6,64]{1,3,2,0:T(8,128)}, f32[2,1024,6,64]{1,3,2,0:T(8,128)}, f32[2,1024,6,64]{1,3,2,0:T(8,128)}, f32[2,1024,6,64]{1,3,2...) fusion(f32[6]{0:T(128)} %get-tuple-element.134, ...), kind=kLoop, calls=%fused_computation.167 | loop fusion | flops 14155776 | bytes 56631704 | tf_op jit(solution)/shard_map/transpose(jvp(vmap()))/mul | solution.py:85
  630.5 34.7 %pad_add_fusion = f32[2,1056,6,64]{1,3,2,0:T(8,128)} fusion(f32[2,1024,6,64]{1,3,2,0:T(8,128)} %get-tuple-element.163, f32[2,1024,6,64]{1,3,2,0:T(8,128)} %get-tuple-element.164, f32[2,1024,6,64]{1,3,2,0:T(8,128)} %get-tuple-element.165, f32[2,1024,6,64]{1,3,2,0:T(8,128)} %get-tuple-element.166, f32[2,1024,6,64]{1,3,2,0:T(8,128)} %get-tuple-element.167, ...), kind=kLoop, calls=%fused_computation.25 | loop fusion | flops 21086208 | bytes 88178688 | tf_op jit(solution)/shard_map/transpose(jvp(vmap()))/add_any | solution.py:85
  665.2 12.1 fusion.12
  691.7 5.0 convolution_bitcast_fusion.1
  706.9 5.2 fusion.74
  712.2 9.6 fusion.175
  721.8 9.7 fusion.172
  734.2 40.9 %all-reduce.75 = (f32[768]{0:T(1024)S(1)}, f32[768]{0:T(1024)S(1)}, f32[768]{0:T(1024)S(1)}, f32[768]{0:T(1024)S(1)}) all-reduce(f32[768]{0:T(1024)S(1)} %copy-done.126, f32[768]{0:T(1024)S(1)} %copy-done.127, f32[768]{0:T(1024)S(1)} %copy-done.124, f32[768]{0:T(1024)S(1)} %copy-done.125), channel_id=9, replica_groups=mesh['dp'=16,'mp'=2] {'dp','mp'}, use_global_device_ids=true, to_apply=%region_65.66.clone | all-reduce | flops 3072 | bytes 24576
  780.4 28.5 %multiply_reduce_fusion.33 = (f32[6]{0:T(128)S(1)}, f32[6]{0:T(128)S(1)}, f32[6]{0:T(128)S(1)}, f32[6]{0:T(128)S(1)}, f32[6]{0:T(128)S(1)}, /*index=5*/f32[6]{0:...) fusion(f32[2,1024,6,64]{1,3,2,0:T(8,128)} %copy-done.4, ...), kind=kLoop, calls=%fused_computation.108 | loop fusion | flops 27525018 | bytes 6300056 | tf_op jit(solution)/shard_map/transpose(jvp(vmap()))/reduce_sum | solution.py:85
  809.1 75.8 %psum.7 = f32[6,33]{0,1:T(8,128)S(1)} all-reduce(f32[6,33]{0,1:T(8,128)S(1)} %pad_add_fusion.7), channel_id=1, replica_groups=mesh['dp'=16,'mp'=2] {'dp'}, use_global_device_ids=true, to_apply=%region_62.63 | all-reduce | flops 198 | bytes 1584 | tf_op jit(solution)/shard_map/psum | solution.py:214
  890.8 66.8 %reduce-scatter.30.cloned.1.call-done = f32[48,384]{1,0:T(8,128)} async-done(((f32[768,384]{1,0:T(8,128)}), f32[48,384]{1,0:T(8,128)}) %reduce-scatter.30.cloned.1.call-update) | async-done | bytes 73744
  957.6 129.3 %reduce-scatter.32.cloned.1.call-done = f32[48,384]{1,0:T(8,128)} async-done(((f32[768,384]{1,0:T(8,128)}), f32[48,384]{1,0:T(8,128)}) %reduce-scatter.32.cloned.1.call-update) | async-done | bytes 73744
  1086.9 104.5 %reduce-scatter.22.cloned.1.call-done = f32[768,24]{0,1:T(8,128)} async-done(((f32[768,768]{0,1:T(8,128)}), f32[768,24]{0,1:T(8,128)}) %reduce-scatter.22.cloned.1.call-update) | async-done | bytes 73744 | tf_op jit(solution)/shard_map/reduce_scatter | solution.py:208
  1191.3 143.0 %reduce-scatter.26.cloned.1.call-done = f32[1536,48]{0,1:T(8,128)} async-done(((f32[1536,768]{0,1:T(8,128)}), f32[1536,48]{0,1:T(8,128)}) %reduce-scatter.26.cloned.1.call-update) | async-done | bytes 294928 | tf_op jit(solution)/shard_map/reduce_scatter | solution.py:205
  1334.3 143.3 %reduce-scatter.24.cloned.1.call-done = f32[48,1536]{1,0:T(8,128)} async-done(((f32[768,1536]{1,0:T(8,128)}), f32[48,1536]{1,0:T(8,128)}) %reduce-scatter.24.cloned.1.call-update) | async-done | bytes 294928 | tf_op jit(solution)/shard_map/reduce_scatter | solution.py:204
  (667 shorter events, 264.5 us)
Async XLA Ops:
  7.2 55.0 %copy-start.204 = (s32[32]{0:T(128)S(1)}, s32[32]{0:T(128)}, u32[]{:S(2)}) copy-start(s32[32]{0:T(128)} %param.26) | copy-start | bytes 388
  7.2 55.1 %copy-start.119 = (bf16[48,384]{1,0:T(8,128)(2,1)S(1)}, bf16[48,384]{1,0:T(8,128)(2,1)}, u32[]{:S(2)}) copy-start(bf16[48,384]{1,0:T(8,128)(2,1)} %param.15) | copy-start | bytes 110596
  7.2 99.1 %copy-start.120 = (bf16[48,384]{1,0:T(8,128)(2,1)S(1)}, bf16[48,384]{1,0:T(8,128)(2,1)}, u32[]{:S(2)}) copy-start(bf16[48,384]{1,0:T(8,128)(2,1)} %param.16) | copy-start | bytes 110596
  7.3 140.2 %copy-start.121 = (bf16[48,384]{1,0:T(8,128)(2,1)S(1)}, bf16[48,384]{1,0:T(8,128)(2,1)}, u32[]{:S(2)}) copy-start(bf16[48,384]{1,0:T(8,128)(2,1)} %param.17) | copy-start | bytes 110596
  7.3 184.5 %all-gather.7.cloned.1.call-start = ((), (), s32[]{:S(2)}) async-start(), calls=%async_computation.11 | async-start | bytes 4718592 | tf_op jit(solution)/shard_map/all_gather | solution.py:129
  8.0 293.3 %all-gather.9.cloned.1.call-start = ((), (), s32[]{:S(2)}) async-start(), calls=%async_computation.12 | async-start | bytes 1216512 | tf_op jit(solution)/shard_map/all_gather | solution.py:118
  8.7 302.8 %all-gather.13.cloned.1.call-start = ((), (), s32[]{:S(2)}) async-start(), calls=%async_computation.14 | async-start | bytes 2506752 | tf_op jit(solution)/shard_map/all_gather | solution.py:114
  62.3 151.3 %copy-start.102 = (pred[2,1024]{1,0:T(4,128)(4,1)}, pred[2,1024]{1,0:T(4,128)(4,1)S(1)}, u32[]{:S(2)}) copy-start(pred[2,1024]{1,0:T(4,128)(4,1)S(1)} %get-tuple-element.190) | copy-start | bytes 6148
  62.4 204.7 %copy-start.94 = (f32[2,1024]{1,0:T(2,128)}, f32[2,1024]{1,0:T(2,128)S(1)}, u32[]{:S(2)}) copy-start(f32[2,1024]{1,0:T(2,128)S(1)} %get-tuple-element.191) | copy-start | bytes 24580
  106.3 94.6 %copy-start.75 = (bf16[768,384]{1,0:T(8,128)(2,1)}, bf16[768,384]{1,0:T(8,128)(2,1)S(1)}, u32[]{:S(2)}) copy-start(bf16[768,384]{1,0:T(8,128)(2,1)S(1)} %all_gather.45) | copy-start | bytes 1769476
  147.4 44.4 %copy-start.77 = (bf16[768,384]{1,0:T(8,128)(2,1)}, bf16[768,384]{1,0:T(8,128)(2,1)S(1)}, u32[]{:S(2)}) copy-start(bf16[768,384]{1,0:T(8,128)(2,1)S(1)} %all_gather.46) | copy-start | bytes 1769476
  216.1 38.6 %copy-start = (f32[2,6,64,1024]{3,2,1,0:T(8,128)}, f32[2,6,64,1024]{3,2,1,0:T(8,128)S(1)}, u32[]{:S(2)}) copy-start(f32[2,6,64,1024]{3,2,1,0:T(8,128)S(1)} %get-tuple-element.195) | copy-start | bytes 9437188
  267.0 30.5 %copy-start.4 = (f32[2,1024,6,64]{1,3,2,0:T(8,128)}, f32[2,1024,6,64]{1,3,2,0:T(8,128)S(1)}, u32[]{:S(2)}) copy-start(f32[2,1024,6,64]{1,3,2,0:T(8,128)S(1)} %copy_multiply_fusion) | copy-start | bytes 9437188
  297.5 6.2 all-to-all-start
  301.2 17.8 %all-gather.11.cloned.1.call-start = ((), (), s32[]{:S(2)}) async-start(), calls=%async_computation.13 | async-start | bytes 4718592 | tf_op jit(solution)/shard_map/all_gather | solution.py:155
  310.9 74.2 %all-gather.15.cloned.1.call-start = ((), (), s32[]{:S(2)}) async-start(), calls=%async_computation.15 | async-start | bytes 2506752 | tf_op jit(solution)/shard_map/all_gather | solution.py:115
  311.5 92.2 %reduce-scatter.16.cloned.1.call-start = ((), (), s32[]{:S(2)}) async-start(), calls=%async_computation.16 | async-start | bytes 4718592 | tf_op jit(solution)/shard_map/reduce_scatter | solution.py:159
  394.2 34.4 %all-gather.17.cloned.1.call-start = ((), (), s32[]{:S(2)}) async-start(), calls=%async_computation.17 | async-start | bytes 4718592 | tf_op jit(solution)/shard_map/all_gather | solution.py:165
  415.1 52.3 %reduce-scatter.18.cloned.1.call-start = ((), (), s32[]{:S(2)}) async-start(), calls=%async_computation.18 | async-start | bytes 4718592 | tf_op jit(solution)/shard_map/reduce_scatter | solution.py:177
  455.1 430.5 %reduce-scatter.20.cloned.1.call-start = ((), (), s32[]{:S(2)}) async-start(), calls=%async_computation.19 | async-start | bytes 4718592 | tf_op jit(solution)/shard_map/reduce_scatter | solution.py:194
  684.1 206.7 %reduce-scatter.28.cloned.1.call-start = ((), (), s32[]{:S(2)}) async-start(), calls=%async_computation.23 | async-start | bytes 1253376
  691.6 266.0 %reduce-scatter.30.cloned.1.call-start = ((), (), s32[]{:S(2)}) async-start(), calls=%async_computation.24 | async-start | bytes 1253376
  699.4 387.5 %reduce-scatter.32.cloned.1.call-start = ((), (), s32[]{:S(2)}) async-start(), calls=%async_computation.25 | async-start | bytes 1253376
  706.9 484.5 %reduce-scatter.22.cloned.1.call-start = ((), (), s32[]{:S(2)}) async-start(), calls=%async_computation.20 | async-start | bytes 2433024 | tf_op jit(solution)/shard_map/reduce_scatter | solution.py:208
  712.1 622.2 %reduce-scatter.26.cloned.1.call-start = ((), (), s32[]{:S(2)}) async-start(), calls=%async_computation.22 | async-start | bytes 5013504 | tf_op jit(solution)/shard_map/reduce_scatter | solution.py:205
  721.8 755.8 %reduce-scatter.24.cloned.1.call-start = ((), (), s32[]{:S(2)}) async-start(), calls=%async_computation.21 | async-start | bytes 5013504 | tf_op jit(solution)/shard_map/reduce_scatter | solution.py:204
  780.3 28.6 %copy-start.187 = (f32[6]{0:T(128)S(1)}, f32[6]{0:T(128)}, u32[]{:S(2)}) copy-start(f32[6]{0:T(128)} %get-tuple-element.85) | copy-start | bytes 76
  780.3 28.6 %copy-start.188 = (f32[6]{0:T(128)S(1)}, f32[6]{0:T(128)}, u32[]{:S(2)}) copy-start(f32[6]{0:T(128)} %get-tuple-element.86) | copy-start | bytes 76
  780.3 28.6 %copy-start.189 = (f32[6]{0:T(128)S(1)}, f32[6]{0:T(128)}, u32[]{:S(2)}) copy-start(f32[6]{0:T(128)} %get-tuple-element.87) | copy-start | bytes 76
  780.3 28.6 %copy-start.190 = (f32[6]{0:T(128)S(1)}, f32[6]{0:T(128)}, u32[]{:S(2)}) copy-start(f32[6]{0:T(128)} %get-tuple-element.88) | copy-start | bytes 76
  780.3 28.6 %copy-start.191 = (f32[6]{0:T(128)S(1)}, f32[6]{0:T(128)}, u32[]{:S(2)}) copy-start(f32[6]{0:T(128)} %get-tuple-element.89) | copy-start | bytes 76
  780.3 28.6 %copy-start.192 = (f32[6]{0:T(128)S(1)}, f32[6]{0:T(128)}, u32[]{:S(2)}) copy-start(f32[6]{0:T(128)} %get-tuple-element.90) | copy-start | bytes 76
  (203 other events, 1192.3 us)
Sparse Core Ops, SparseCore 0:
  9.6 14.8 all-gather.6
  27.4 56.4 all-gather.8
  86.7 69.3 all-gather.12
  311.0 8.0 all-gather.10
  321.7 63.3 all-gather.14
  394.3 9.3 reduce-scatter.15
  415.2 13.3 all-gather.16
  455.2 12.1 reduce-scatter.17
  684.2 12.2 reduce-scatter.19
  701.7 126.3 reduce-scatter.27
  833.4 124.1 reduce-scatter.29
  962.8 124.0 reduce-scatter.31
  1092.7 98.5 reduce-scatter.21
  1196.9 137.3 reduce-scatter.25
  1339.9 137.6 reduce-scatter.23
where the time goes:
time: 1490 us; the launch traced here: 1480 us
  waiting for transfers between devices  658 us (44%)
  blocking collectives  293 us (20%)
  matrix products  288 us (19%)
  other arithmetic  154 us (10%)
  local copies, waits for them, and re-layouts  70.2 us (5%)
  between operations  17.8 us (1%)
    unnamed x18, waiting for transfers between devices  199 us
    reduce_scatter x1, waiting for transfers between devices, on_device(): lax.psum_scatter(expand_grad, 'dp', scatter_dimension=0, tiled=True)  143 us
    reduce_scatter x1, waiting for transfers between devices, on_device(): lax.psum_scatter(shrink_grad, 'dp', scatter_dimension=1, tiled=True)  143 us
    reduce_scatter x1, waiting for transfers between devices, on_device(): lax.psum_scatter(output_grad, ('dp', 'mp'), scatter_dimension=1, tiled=True)  104 us
    unnamed x2, blocking collectives  83 us
    psum x1, blocking collectives, on_device(): taps_grad = lax.psum(taps_grad, 'dp')  75.8 us
    dot_general x6, matrix products, ahead(): return jnp.dot(left, right, preferred_element_type=jnp.float32)  60.9 us
    reduce_sum x4, other arithmetic, nystrom(): mixed = mixed + taps[:, index][None, :, None] * padded[index:index + slots]  46.4 us
  transfers between devices with their start and end apart: 16, of which 11 were waited for; matrix products, arithmetic and copies ran while one was open for 17% of the time, Pallas kernels for 0%

commit v1 on v0

--- a/solution.py
+++ b/solution.py
@@ -1,3 +1,4 @@
+import functools
 import jax
 import jax.numpy as jnp
 from jax import lax
@@ -8,6 +9,24 @@
 KERNEL = 33
 PINV_STEPS = 6
 HIGH = lax.Precision.HIGHEST
+
+
+def _take_field(inner_x, peer_axis):
+    a_now, y2, part_now = (lax.axis_size(peer_axis), lax.axis_index(peer_axis), inner_x.shape[0])
+    queue = tuple(((c, (c + 1) % a_now) for c in range(a_now)))
+    x_next = jnp.zeros((*inner_x.shape[:0], a_now * part_now, *inner_x.shape[1:]), inner_x.dtype)
+    far_arr = inner_x
+    dev_j = 0
+    while dev_j < a_now:
+        local_now = (y2 - dev_j) % a_now
+        x_next = lax.dynamic_update_slice_in_dim(x_next, far_arr, local_now * part_now, axis=0)
+        if dev_j < a_now - 1:
+            far_arr = lax.ppermute(far_arr, peer_axis, queue)
+        dev_j += 1
+    return x_next
+
+
+sides_state = functools.partial(_take_field, peer_axis="dp")
 
 
 def ahead(left, right):
@@ -108,7 +127,7 @@
     slots = tokens.shape[0]
     pair = lax.dynamic_slice_in_dim(doc_lengths, group * parts, parts)
     full_query, full_keys, full_values, full_expand, full_shrink = (
-        lax.all_gather(w_query, "dp", axis=0, tiled=True),
+        sides_state(w_query),
         lax.all_gather(w_key, "dp", axis=0, tiled=True),
         lax.all_gather(w_value, "dp", axis=0, tiled=True),
         lax.all_gather(w_expand, "dp", axis=0, tiled=True),

time: 1490 us -> 1580 us (1.060)
  waiting for transfers between devices: 658 us -> 751 us
    ppermute x0 -> x15, waiting for transfers between devices: none -> 103 us  [_take_field(): far_arr = lax.ppermute(far_arr, peer_axis, queue)]
    unnamed x461 -> x455, local copies, waits for them, and re-layouts: 37.1 us -> 37.4 us
  transfers between devices with their start and end apart: 16 -> 31, of which waited for: 11 -> 24; matrix products, arithmetic and copies ran while one was open for 17% -> 16% of each run, Pallas kernels for 0% -> 0%
where the time goes in v1:
time: 1580 us
  waiting for transfers between devices  751 us (48%)
  blocking collectives  291 us (18%)
  matrix products  284 us (18%)
  other arithmetic  154 us (10%)
  local copies, waits for them, and re-layouts  69.6 us (4%)
  between operations  17.8 us (1%)
    unnamed x18, waiting for transfers between devices  197 us
    reduce_scatter x1, waiting for transfers between devices, on_device(): lax.psum_scatter(expand_grad, 'dp', scatter_dimension=0, tiled=True)  143 us
    reduce_scatter x1, waiting for transfers between devices, on_device(): lax.psum_scatter(shrink_grad, 'dp', scatter_dimension=1, tiled=True)  143 us
    reduce_scatter x1, waiting for transfers between devices, on_device(): lax.psum_scatter(output_grad, ('dp', 'mp'), scatter_dimension=1, tiled=True)  105 us
    ppermute x15, waiting for transfers between devices, _take_field(): far_arr = lax.ppermute(far_arr, peer_axis, queue)  103 us
    psum x1, blocking collectives, on_device(): taps_grad = lax.psum(taps_grad, 'dp')  75.2 us
    unnamed x2, blocking collectives  75.2 us
    dot_general x6, matrix products, ahead(): return jnp.dot(left, right, preferred_element_type=jnp.float32)  61.1 us
  transfers between devices with their start and end apart: 31, of which 24 were waited for; matrix products, arithmetic and copies ran while one was open for 16% of the time, Pallas kernels for 0%

profile of v1, /device:TPU:0, one launch (start us, length us, event | category | flops | bytes accessed | tf_op | source)
XLA Modules:
  0.0 1577.0 jit_solution(14431891282919995556)
XLA Ops:
  16.4 47.0 %all_gather.44 = bf16[768,384]{1,0:T(8,128)(2,1)} all-gather(bf16[48,384]{1,0:T(8,128)(2,1)} %param.16), channel_id=1, replica_groups=mesh['dp'=16,'mp'=2] {'dp'}, dimensions={0}, use_global_device_ids=true | all-gather | bytes 626688 | tf_op jit(solution)/shard_map/all_gather | solution.py:131
  63.4 42.3 %all_gather.45 = bf16[768,384]{1,0:T(8,128)(2,1)} all-gather(bf16[48,384]{1,0:T(8,128)(2,1)} %param.17), channel_id=1, replica_groups=mesh['dp'=16,'mp'=2] {'dp'}, dimensions={0}, use_global_device_ids=true | all-gather | bytes 626688 | tf_op jit(solution)/shard_map/all_gather | solution.py:132
  110.0 38.0 %all-reduce.76 = (bf16[768]{0:T(1024)(128)(2,1)S(1)}, bf16[768]{0:T(1024)(128)(2,1)S(1)}, bf16[768]{0:T(1024)(128)(2,1)}, bf16[768]{0:T(1024)(128)(2,1)}) all-reduce(bf16[768]{0:T(1024)(128)(2,1)S(1)} %dynamic-update-slice.1, bf16[768]{0:T(1024)(128)(2,1)S(1)} %dynamic-update-slice, ...), channel_id=1, replica_groups=mesh['dp'=16,'mp'=2] {'dp','mp'}, use_global_device_ids=true, to_apply=%add.68 | all-reduce | flops 3072 | bytes 12288
  156.8 7.5 collective-permute-done.2
  164.4 7.5 collective-permute-done.3
  179.5 7.5 collective-permute-done.5
  187.0 7.7 collective-permute-done.6
  194.7 7.5 collective-permute-done.7
  232.5 7.5 collective-permute-done.12
  240.1 7.5 collective-permute-done.13
  329.5 29.7 %multiply_convert_fusion.1 = bf16[2,1024,6,64]{1,3,2,0:T(8,128)(2,1)} fusion(f32[2,1024,6,64]{1,3,2,0:T(8,128)S(1)} %copy_multiply_fusion, f32[2,6,64,64]{3,2,1,0:T(8,128)S(1)} %fusion.158, f32[6]{0:T(128)S(1)} %copy-done.153, f32[6]{0:T(128)S(1)} %copy-done.180, f32[6]{0:T(128)S(1)} %copy-done.154, f32[6]{0:T(128)S(1)} %copy-done.156, ...), kind=kOutput, calls=%fused_computation.121 | convolution fusion | flops 659816448 | bytes 8168216 | tf_op jit(solution)/shard_map/jvp(vmap(hsj,hjd->shd))/dot_general | solution.py:100
  380.7 35.5 %multiply_convert_fusion = (bf16[2048,1536]{1,0:T(8,128)(2,1)}, f32[2048,1536]{1,0:T(8,128)}, f32[2048,1536]{1,0:T(8,128)}) fusion(bf16[2048,768]{0,1:T(8,128)(2,1)} %all-gather.11.cloned.1.call-done, bf16[768,1536]{1,0:T(8,128)(2,1)} %all-gather.13.cloned.1.call-done), kind=kOutput, calls=%fused_computation.3 | convolution fusion | flops 5036310528 | bytes 36962304 | tf_op jit(solution)/shard_map/dot_general | solution.py:33
  416.2 30.5 %all-gather.15.cloned.1.call-done = bf16[1536,768]{0,1:T(8,128)(2,1)} async-done(((bf16[1536,48]{0,1:T(8,128)(2,1)}), bf16[1536,768]{0,1:T(8,128)(2,1)}) %all-gather.15.cloned.1.call-update) | async-done | bytes 2359312 | tf_op jit(solution)/shard_map/all_gather | solution.py:134
  446.8 9.0 convolution_convert_fusion.1
  476.8 13.5 all-gather.17.cloned.1.call-done
  490.2 17.3 %add_convert_fusion = bf16[2048,1536]{1,0:T(8,128)(2,1)S(1)} fusion(f32[2048,1536]{1,0:T(8,128)} %get-tuple-element.153, f32[2048,1536]{1,0:T(8,128)} %get-tuple-element.200, bf16[2048,768]{0,1:T(8,128)(2,1)} %all-gather.17.cloned.1.call-done, bf16[1536,768]{0,1:T(8,128)(2,1)} %all-gather.15.cloned.1.call-done), kind=kOutput, calls=%fused_computation.2 | convolution fusion | flops 4875878400 | bytes 36962304 | tf_op jit(solution)/shard_map/dot_general | solution.py:37
  517.4 46.4 %all_gather.55 = bf16[768,384]{1,0:T(8,128)(2,1)} all-gather(bf16[48,384]{1,0:T(8,128)(2,1)S(1)} %copy-done.111), channel_id=1, replica_groups=mesh['dp'=16,'mp'=2] {'dp'}, dimensions={0}, use_global_device_ids=true | all-gather | bytes 626688 | tf_op jit(solution)/shard_map/all_gather | solution.py:186
  634.2 15.2 multiply_reduce_fusion.32
  649.6 16.9 %broadcast_multiply_fusion.1 = (f32[2,1024,6,64]{1,3,2,0:T(8,128)}, f32[2,1024,6,64]{1,3,2,0:T(8,128)}, f32[2,1024,6,64]{1,3,2,0:T(8,128)}, f32[2,1024,6,64]{1,3...) fusion(f32[6]{0:T(128)S(1)} %copy-done.181, ...), kind=kLoop, calls=%fused_computation.169 | loop fusion | flops 11796480 | bytes 47194448 | tf_op jit(solution)/shard_map/transpose(jvp(vmap()))/mul | solution.py:104
  666.5 21.3 %broadcast_multiply_fusion = (f32[2,1024,6,64]{1,3,2,0:T(8,128)}, f32[2,1024,6,64]{1,3,2,0:T(8,128)}, f32[2,1024,6,64]{1,3,2,0:T(8,128)}, f32[2,1024,6,64]{1,3,2...) fusion(f32[6]{0:T(128)} %get-tuple-element.134, ...), kind=kLoop, calls=%fused_computation.168 | loop fusion | flops 14155776 | bytes 56631704 | tf_op jit(solution)/shard_map/transpose(jvp(vmap()))/mul | solution.py:104
  727.2 34.6 %pad_add_fusion = f32[2,1056,6,64]{1,3,2,0:T(8,128)} fusion(f32[2,1024,6,64]{1,3,2,0:T(8,128)} %get-tuple-element.163, f32[2,1024,6,64]{1,3,2,0:T(8,128)} %get-tuple-element.164, f32[2,1024,6,64]{1,3,2,0:T(8,128)} %get-tuple-element.165, f32[2,1024,6,64]{1,3,2,0:T(8,128)} %get-tuple-element.166, f32[2,1024,6,64]{1,3,2,0:T(8,128)} %get-tuple-element.167, ...), kind=kLoop, calls=%fused_computation.25 | loop fusion | flops 21086208 | bytes 88178688 | tf_op jit(solution)/shard_map/transpose(jvp(vmap()))/add_any | solution.py:104
  761.8 12.0 fusion.12
  810.9 9.8 fusion.176
  820.8 9.6 fusion.173
  833.0 37.1 %all-reduce.75 = (f32[768]{0:T(1024)S(1)}, f32[768]{0:T(1024)S(1)}, f32[768]{0:T(1024)S(1)}, f32[768]{0:T(1024)S(1)}) all-reduce(f32[768]{0:T(1024)S(1)} %copy-done.126, f32[768]{0:T(1024)S(1)} %copy-done.127, f32[768]{0:T(1024)S(1)} %copy-done.124, f32[768]{0:T(1024)S(1)} %copy-done.125), channel_id=9, replica_groups=mesh['dp'=16,'mp'=2] {'dp','mp'}, use_global_device_ids=true, to_apply=%region_65.66.clone | all-reduce | flops 3072 | bytes 24576
  875.4 28.5 %multiply_reduce_fusion.33 = (f32[6]{0:T(128)S(1)}, f32[6]{0:T(128)S(1)}, f32[6]{0:T(128)S(1)}, f32[6]{0:T(128)S(1)}, f32[6]{0:T(128)S(1)}, /*index=5*/f32[6]{0:...) fusion(f32[2,1024,6,64]{1,3,2,0:T(8,128)} %copy-done.4, ...), kind=kLoop, calls=%fused_computation.108 | loop fusion | flops 27525018 | bytes 6300056 | tf_op jit(solution)/shard_map/transpose(jvp(vmap()))/reduce_sum | solution.py:104
  904.1 75.2 %psum.7 = f32[6,33]{0,1:T(8,128)S(1)} all-reduce(f32[6,33]{0,1:T(8,128)S(1)} %pad_add_fusion.7), channel_id=1, replica_groups=mesh['dp'=16,'mp'=2] {'dp'}, use_global_device_ids=true, to_apply=%region_62.63 | all-reduce | flops 198 | bytes 1584 | tf_op jit(solution)/shard_map/psum | solution.py:233
  985.2 65.3 %reduce-scatter.30.cloned.1.call-done = f32[48,384]{1,0:T(8,128)} async-done(((f32[768,384]{1,0:T(8,128)}), f32[48,384]{1,0:T(8,128)}) %reduce-scatter.30.cloned.1.call-update) | async-done | bytes 73744
  1050.5 129.4 %reduce-scatter.32.cloned.1.call-done = f32[48,384]{1,0:T(8,128)} async-done(((f32[768,384]{1,0:T(8,128)}), f32[48,384]{1,0:T(8,128)}) %reduce-scatter.32.cloned.1.call-update) | async-done | bytes 73744
  1179.9 104.5 %reduce-scatter.22.cloned.1.call-done = f32[768,24]{0,1:T(8,128)} async-done(((f32[768,768]{0,1:T(8,128)}), f32[768,24]{0,1:T(8,128)}) %reduce-scatter.22.cloned.1.call-update) | async-done | bytes 73744 | tf_op jit(solution)/shard_map/reduce_scatter | solution.py:227
  1284.4 142.8 %reduce-scatter.26.cloned.1.call-done = f32[1536,48]{0,1:T(8,128)} async-done(((f32[1536,768]{0,1:T(8,128)}), f32[1536,48]{0,1:T(8,128)}) %reduce-scatter.26.cloned.1.call-update) | async-done | bytes 294928 | tf_op jit(solution)/shard_map/reduce_scatter | solution.py:224
  1427.2 143.1 %reduce-scatter.24.cloned.1.call-done = f32[48,1536]{1,0:T(8,128)} async-done(((f32[768,1536]{1,0:T(8,128)}), f32[48,1536]{1,0:T(8,128)}) %reduce-scatter.24.cloned.1.call-update) | async-done | bytes 294928 | tf_op jit(solution)/shard_map/reduce_scatter | solution.py:223
  (706 shorter events, 351.5 us)
Async XLA Ops:
  7.2 248.0 %all-gather.7.cloned.1.call-start = ((), (), s32[]{:S(2)}) async-start(), calls=%async_computation.11 | async-start | bytes 4718592 | tf_op jit(solution)/shard_map/all_gather | solution.py:148
  8.0 354.9 %all-gather.9.cloned.1.call-start = ((), (), s32[]{:S(2)}) async-start(), calls=%async_computation.12 | async-start | bytes 1216512 | tf_op jit(solution)/shard_map/all_gather | solution.py:137
  8.7 364.4 %all-gather.13.cloned.1.call-start = ((), (), s32[]{:S(2)}) async-start(), calls=%async_computation.14 | async-start | bytes 2506752 | tf_op jit(solution)/shard_map/all_gather | solution.py:133
  8.8 140.5 %collective-permute-start = (bf16[48,384]{1,0:T(8,128)(2,1)}, bf16[48,384]{1,0:T(8,128)(2,1)S(1)}, u32[]{:S(2)}, u32[]{:S(2)}) collective-permute-start(bf16[48,384]{1,0:T(8,128)(2,1)} %param.15), channel_id=1, source_target_pairs={{0,2},{2,4},{4,6},{6,8},{8,10},{10,12},{12,14},{14,16},{16,18},{18... | collective-permute-start | bytes 110600 | tf_op jit(solution)/shard_map/ppermute | solution.py:24
  16.4 312.3 %copy-start.95 = (f32[2,1024]{1,0:T(2,128)}, f32[2,1024]{1,0:T(2,128)S(1)}, u32[]{:S(2)}) copy-start(f32[2,1024]{1,0:T(2,128)S(1)} %get-tuple-element.191) | copy-start | bytes 24580
  149.2 7.6 collective-permute-start.1
  156.8 7.6 collective-permute-start.2
  164.3 7.6 collective-permute-start.3
  171.9 7.6 collective-permute-start.4
  179.5 7.6 collective-permute-start.5
  187.0 7.7 collective-permute-start.6
  194.7 7.6 collective-permute-start.7
  202.3 7.6 collective-permute-start.8
  209.8 7.6 collective-permute-start.9
  217.4 7.6 collective-permute-start.10
  224.9 7.6 collective-permute-start.11
  232.5 7.6 collective-permute-start.12
  240.1 7.6 collective-permute-start.13
  247.6 7.6 collective-permute-start.14
  359.1 6.2 all-to-all-start
  362.8 17.9 %all-gather.11.cloned.1.call-start = ((), (), s32[]{:S(2)}) async-start(), calls=%async_computation.13 | async-start | bytes 4718592 | tf_op jit(solution)/shard_map/all_gather | solution.py:174
  372.5 74.2 %all-gather.15.cloned.1.call-start = ((), (), s32[]{:S(2)}) async-start(), calls=%async_computation.15 | async-start | bytes 2506752 | tf_op jit(solution)/shard_map/all_gather | solution.py:134
  373.1 92.2 %reduce-scatter.16.cloned.1.call-start = ((), (), s32[]{:S(2)}) async-start(), calls=%async_computation.16 | async-start | bytes 4718592 | tf_op jit(solution)/shard_map/reduce_scatter | solution.py:178
  455.8 34.4 %all-gather.17.cloned.1.call-start = ((), (), s32[]{:S(2)}) async-start(), calls=%async_computation.17 | async-start | bytes 4718592 | tf_op jit(solution)/shard_map/all_gather | solution.py:184
  476.7 90.7 %reduce-scatter.18.cloned.1.call-start = ((), (), s32[]{:S(2)}) async-start(), calls=%async_computation.18 | async-start | bytes 4718592 | tf_op jit(solution)/shard_map/reduce_scatter | solution.py:196
  516.7 463.3 %reduce-scatter.20.cloned.1.call-start = ((), (), s32[]{:S(2)}) async-start(), calls=%async_computation.19 | async-start | bytes 4718592 | tf_op jit(solution)/shard_map/reduce_scatter | solution.py:213
  782.5 202.7 %reduce-scatter.28.cloned.1.call-start = ((), (), s32[]{:S(2)}) async-start(), calls=%async_computation.23 | async-start | bytes 1253376
  790.6 259.9 %reduce-scatter.30.cloned.1.call-start = ((), (), s32[]{:S(2)}) async-start(), calls=%async_computation.24 | async-start | bytes 1253376
  798.1 381.8 %reduce-scatter.32.cloned.1.call-start = ((), (), s32[]{:S(2)}) async-start(), calls=%async_computation.25 | async-start | bytes 1253376
  805.6 478.8 %reduce-scatter.22.cloned.1.call-start = ((), (), s32[]{:S(2)}) async-start(), calls=%async_computation.20 | async-start | bytes 2433024 | tf_op jit(solution)/shard_map/reduce_scatter | solution.py:227
  810.9 616.4 %reduce-scatter.26.cloned.1.call-start = ((), (), s32[]{:S(2)}) async-start(), calls=%async_computation.22 | async-start | bytes 5013504 | tf_op jit(solution)/shard_map/reduce_scatter | solution.py:224
  820.7 749.6 %reduce-scatter.24.cloned.1.call-start = ((), (), s32[]{:S(2)}) async-start(), calls=%async_computation.21 | async-start | bytes 5013504 | tf_op jit(solution)/shard_map/reduce_scatter | solution.py:223
  (215 other events, 2833.9 us)
Sparse Core Ops, SparseCore 0:
  9.6 14.8 all-gather.6
  27.3 56.0 all-gather.8
  86.2 62.9 all-gather.12
  372.6 8.0 all-gather.10
  383.3 63.3 all-gather.14
  455.9 9.3 reduce-scatter.15
  476.8 13.3 all-gather.16
  516.8 12.1 reduce-scatter.17
  782.6 6.8 reduce-scatter.19
  794.6 126.3 reduce-scatter.27
  926.4 124.0 reduce-scatter.29
  1055.7 124.1 reduce-scatter.31
  1185.7 98.6 reduce-scatter.21
  1290.0 137.1 reduce-scatter.25
  1432.8 137.4 reduce-scatter.23
